TPU v7x, 32 devices: a whole 2x2x4 slice. The times are simulated.
32 devices in a mesh: samp: 8 (over y, x, core), par: 4 (over z).
Axes of the slice: x: 2, y: 2, z: 4, core: 2. Of those that a mesh axis runs over, the one named last changes fastest.
Arguments:
- log_derivs: bfloat16 [512, 262144], P('samp', 'par')
- energies: float32 [512, 8], P('samp'), may hold values from -6 to 6
- nys_rows: int32 [8, 8], P('samp'), may hold values from 0 to 63, as said below
Outputs:
- update: float32 [262144, 8], P('par')
- solution: float32 [512, 8], P('samp')
Inputs may be any that keep to these rules, and one draw needn't show every extreme that they name: `nys_rows`: each row holds 8 different local sample numbers of that group.
All inputs are finite; a program needn't handle non-finite values.
Results may differ from a plain program's by a relative error of at most 0.014.
Values may be sent and summed in bfloat16 or wider, within the bound.
A program may use at most 128 MiB of HBM per device.

v0:
```python
import math
import jax
import jax.numpy as jnp
from jax import lax
from jax.sharding import PartitionSpec as P

ITERS = 2
damping = 0.5


def factor_solve(factor, right):
    middle = lax.linalg.triangular_solve(factor, right, left_side=True, lower=True)
    return lax.linalg.triangular_solve(factor, middle, left_side=True, lower=True, transpose_a=True)


def small_solve(matrix, right):
    return factor_solve(jnp.linalg.cholesky(matrix), right)


def hdot(left, right):
    return jnp.dot(left, right, precision=lax.Precision.HIGHEST)


def gram_body(log_derivs, energies, nys_rows):
    samp_rows = log_derivs.shape[0]
    groups = lax.axis_size("samp")
    total_rows = samp_rows * groups
    total_cols = log_derivs.shape[1] * lax.axis_size("par")
    slab = lax.all_to_all(log_derivs, "samp", split_axis=1, concat_axis=0, tiled=True)
    widened = slab.astype(jnp.float32)
    col_mean = jnp.sum(widened, axis=0) / total_rows
    centered = ((widened - col_mean) * (1.0 / math.sqrt(total_cols))).astype(jnp.bfloat16)
    gram = lax.psum(
        jnp.einsum("rc,kc->rk", centered, centered, preferred_element_type=jnp.float32),
        ("samp", "par"),
    )
    all_energies = lax.all_gather(energies, "samp", axis=0, tiled=True)
    all_picks = lax.all_gather(nys_rows, "samp", axis=0, tiled=True)
    selected = (jnp.arange(groups, dtype=jnp.int32)[:, None] * samp_rows + all_picks).reshape(-1)
    sketch = jnp.take(gram, selected, axis=1)
    core_block = jnp.take(sketch, selected, axis=0)
    factor = jnp.linalg.cholesky(damping * core_block + hdot(sketch.T, sketch))

    def precondition(residual):
        coeffs = factor_solve(factor, hdot(sketch.T, residual))
        result = (residual - hdot(sketch, coeffs)) / damping
        return (result, hdot(result.T, residual))

    solution = jnp.zeros(all_energies.shape, jnp.float32)
    residual = all_energies
    precond_res, inner_prev = precondition(residual)
    direction = precond_res
    for iteration in range(ITERS):
        rounded = direction.astype(jnp.bfloat16).astype(jnp.float32)
        image_k = hdot(gram, rounded) + damping * direction
        curvature = hdot(direction.T, image_k)
        alpha_k = small_solve(curvature, inner_prev)
        solution = solution + hdot(direction, alpha_k)
        if iteration + 1 < ITERS:
            residual = residual - hdot(image_k, alpha_k)
            precond_res, inner_next = precondition(residual)
            beta_k = small_solve(inner_prev, inner_next)
            direction = precond_res + hdot(direction, beta_k)
            inner_prev = inner_next
    rounded_sol = solution.astype(jnp.bfloat16)
    local_update = jnp.einsum(
        "rc,rv->cv", centered, rounded_sol, preferred_element_type=jnp.float32
    )
    update = lax.all_gather(local_update.astype(jnp.bfloat16), "samp", axis=0, tiled=True).astype(
        local_update.dtype
    )
    start = lax.axis_index("samp") * samp_rows
    return (update, lax.dynamic_slice_in_dim(solution, start, samp_rows, 0))


def body(log_derivs, energies, nys_rows):
    update, solution = gram_body(log_derivs, energies, nys_rows)
    return (update, solution)


def solution(mesh):
    return jax.shard_map(
        body,
        mesh=mesh,
        in_specs=(P("samp", "par"), P("samp", None), P("samp", None)),
        out_specs=(P("par", None), P("samp", None)),
        check_vma=False,
    )
```

profile of v0, /device:TPU:0, one launch (start us, length us, event | category | flops | bytes accessed | tf_op | source)
XLA Modules:
  0.0 351.4 jit_solution(1456690422608163181)
XLA Ops:
  7.2 7.6 %copy.62 = bf16[8,8,8,8192]{3,2,0,1:T(8,128)(2,1)} copy(bf16[8,8,8,8192]{3,2,1,0:T(8,128)(2,1)} %bitcast.122) | data formatting | bytes 16777216 | tf_op jit(solution)/shard_map/all_to_all | solution.py:29
  14.8 5.3 %all-to-all-start = ((bf16[64,8,8192]{2,0,1:T(8,128)(2,1)}), bf16[64,8,8192]{2,0,1:T(8,128)(2,1)}, u32[]{:S(2)}, u32[]{:S(2)}) async-start(bf16[64,8,8192]{2,0,1:T(8,128)(2,1)} %bitcast.121), calls=%async_computation | async-start | bytes 16777216 | tf_op jit(solution)/shard_map/all_to_all | solution.py:29
  20.1 97.4 %all-gather.1 = s32[8,1,8]{2,1,0:T(1,128)S(1)} all-gather(s32[1,1,8]{2,1,0:T(1,128)S(1)} %bitcast.126), channel_id=1, replica_groups=mesh['samp'=8,'par'=4] {'samp'}, dimensions={0}, use_global_device_ids=true | all-gather | bytes 288 | tf_op jit(solution)/shard_map/all_gather | solution.py:38
  117.7 8.3 %all-gather = f32[8,64,8]{1,2,0:T(8,128)S(1)} all-gather(f32[1,64,8]{1,2,0:T(8,128)S(1)} %bitcast.125), channel_id=1, replica_groups=mesh['samp'=8,'par'=4] {'samp'}, dimensions={0}, use_global_device_ids=true | all-gather | bytes 18432 | tf_op jit(solution)/shard_map/all_gather | solution.py:37
  126.1 5.5 %convert_reduce_fusion = f32[8192]{0:T(1024)S(1)} fusion(bf16[64,8,8192]{2,0,1:T(8,128)(2,1)} %all-to-all-done), kind=kLoop, calls=%fused_computation.8 | loop fusion | flops 8380416 | bytes 8421376 | tf_op jit(solution)/shard_map/reduce_sum | solution.py:31
  131.6 8.9 %multiply_convert_fusion = bf16[64,8,8192]{2,0,1:T(8,128)(2,1)} fusion(bf16[64,8,8192]{2,0,1:T(8,128)(2,1)} %all-to-all-done, f32[8192]{0:T(1024)S(1)} %broadcast_multiply_fusion), kind=kLoop, calls=%fused_computation.5 | loop fusion | flops 16777216 | bytes 16809984 | tf_op jit(solution)/shard_map/convert.2
  140.5 11.3 %fusion.73 = f32[512,512]{1,0:T(8,128)} fusion(bf16[512,8192]{1,0:T(8,128)(2,1)} %bitcast.123), kind=kOutput, calls=%fused_computation.118 | convolution fusion | flops 4294967296 | bytes 9437184 | tf_op jit(solution)/shard_map/rc,kc->rk/dot_general | solution.py:34
  152.0 8.9 %fusion.1 = bf16[512,8192]{1,0:T(8,128)(2,1)} fusion(bf16[64,8,8192]{2,0,1:T(8,128)(2,1)} %all-to-all-done, f32[8192]{0:T(1024)S(1)} %broadcast_multiply_fusion), kind=kLoop, calls=%fused_computation.4 | loop fusion | flops 16777216 | bytes 16809984 | tf_op jit(solution)/shard_map/convert_element_type | solution.py:32
  160.9 122.7 %all-reduce.2.cloned.1.call-done = f32[512,512]{1,0:T(8,128)} async-done(((f32[512,512]{1,0:T(8,128)}), f32[512,512]{1,0:T(8,128)}) %all-reduce.2.cloned.1.call-update) | async-done | bytes 1048592 | tf_op jit(solution)/shard_map/psum | solution.py:33
  283.6 1.6 copy.48
  285.2 0.7 gather_fusion
  287.2 5.8 %cholesky.33 = f32[64,64]{1,0:T(8,128)S(1)} custom-call(f32[64,64]{1,0:T(8,128)S(1)} %fusion.29), custom_call_target="Cholesky" | custom-call | tf_op jit(solution)/shard_map/jit(cholesky)/cholesky | solution.py:42
  293.1 0.6 compare_reduce_fusion.3
  293.7 0.7 fusion.20
  294.4 4.9 %custom-call.24 = f32[1,64,64]{1,2,0:T(8,128)S(1)} custom-call(f32[1,64,64]{2,1,0:T(8,128)S(1)} %fusion.20), custom_call_target="InvertDiagBlocksLowerTriangular" | custom-call | tf_op jit(solution)/shard_map/triangular_solve/custom-call.3 | solution.py:13
  300.4 1.8 convolution_add_fusion.4
  302.4 0.7 cholesky.94
  303.2 0.6 compare_reduce_fusion.2
  303.8 0.6 fusion.44
  304.5 0.6 custom-call.26
  305.9 0.7 cholesky.105
  306.6 0.6 compare_reduce_fusion.1
  307.3 0.6 fusion.45
  307.9 0.6 custom-call.30
  310.9 0.7 cholesky.116
  311.7 0.6 compare_reduce_fusion
  312.4 0.6 fusion.46
  313.0 0.6 custom-call.32
  314.2 5.2 %convolution_convert_fusion = bf16[8192,8]{0,1:T(8,128)(2,1)} fusion(bf16[512,8192]{1,0:T(8,128)(2,1)} %fusion.1, f32[512,8]{0,1:T(8,128)S(1)} %convolution_add_fusion.1), kind=kOutput, calls=%fused_computation.6 | convolution fusion | flops 67178496 | bytes 8536064 | tf_op jit(solution)/shard_map/rc,rv->cv/dot_general | solution.py:66
  319.5 0.7 constant_dynamic-slice_fusion
  320.1 21.8 %all-gather.4.cloned.1.call-done = bf16[65536,8]{0,1:T(8,128)(2,1)} async-done(((bf16[8192,8]{0,1:T(8,128)(2,1)}), bf16[65536,8]{0,1:T(8,128)(2,1)}) %all-gather.4.cloned.1.call-update) | async-done | bytes 1048592 | tf_op jit(solution)/shard_map/all_gather | solution.py:69
  341.9 2.7 convert_element_type.49
  (60 shorter events, 7.1 us)
Async XLA Ops:
  14.8 5.4 %copy-start.2 = (s32[1,8]{1,0:T(1,128)S(1)}, s32[1,8]{1,0:T(1,128)}, u32[]{:S(2)}) copy-start(s32[1,8]{1,0:T(1,128)} %param.14) | copy-start | bytes 100
  14.8 103.0 %copy-start.1 = (f32[64,8]{0,1:T(8,128)S(1)}, f32[64,8]{0,1:T(8,128)}, u32[]{:S(2)}) copy-start(f32[64,8]{0,1:T(8,128)} %param.13) | copy-start | bytes 6148
  14.8 111.4 %all-to-all-start = ((bf16[64,8,8192]{2,0,1:T(8,128)(2,1)}), bf16[64,8,8192]{2,0,1:T(8,128)(2,1)}, u32[]{:S(2)}, u32[]{:S(2)}) async-start(bf16[64,8,8192]{2,0,1:T(8,128)(2,1)} %bitcast.121), calls=%async_computation | async-start | bytes 16777216 | tf_op jit(solution)/shard_map/all_to_all | solution.py:29
  20.1 263.5 %all-reduce.2.cloned.1.call-start = ((), (), s32[]{:S(2)}) async-start(), calls=%async_computation.1 | async-start | bytes 2097152 | tf_op jit(solution)/shard_map/psum | solution.py:33
  151.8 190.1 %all-gather.4.cloned.1.call-start = ((), (), s32[]{:S(2)}) async-start(), calls=%async_computation.2 | async-start | bytes 1179648 | tf_op jit(solution)/shard_map/all_gather | solution.py:69
  283.6 26.5 %copy-start = (f32[512,512]{1,0:T(8,128)S(1)}, f32[512,512]{1,0:T(8,128)}, u32[]{:S(2)}) copy-start(f32[512,512]{1,0:T(8,128)} %all-reduce.2.cloned.1.call-done) | copy-start | bytes 3145732
Sparse Core Ops, SparseCore 0:
  151.9 131.6 all-reduce.1
  319.6 22.3 all-gather.3
where the time goes:
time: 352 us; the launch traced here: 351 us
  waiting for transfers between devices  145 us (41%)
  blocking collectives  106 us (30%)
  other arithmetic  46.2 us (13%)
  matrix products  23.4 us (7%)
  between operations  14.2 us (4%)
  local copies, waits for them, and re-layouts  11.8 us (3%)
  starting transfers between devices  5.59 us (2%)
    psum x1, waiting for transfers between devices, gram_body(): lax.psum(jnp.einsum('rc,kc->rk', centered, centered, preferred_element_ty...  123 us
    all_gather x1, blocking collectives, gram_body(): all_picks = lax.all_gather(nys_rows, 'samp', axis=0, tiled=True)  97.4 us
    all_gather x1, waiting for transfers between devices, gram_body(): lax.all_gather(local_update.astype(jnp.bfloat16), 'samp', axis=0, tiled=T...  21.8 us
    dot_general x1, matrix products, gram_body(): jnp.einsum('rc,kc->rk', centered, centered, preferred_element_type=jnp.fl...  11.3 us
    another operation x8, other arithmetic, factor_solve(): lax.linalg.triangular_solve(factor, middle, left_side=True, lower=True, t...  9.37 us
    another operation x1, other arithmetic  8.89 us
    convert_element_type x1, other arithmetic, gram_body(): ((widened - col_mean) * (1.0 / math.sqrt(total_cols))).astype(jnp.bfloat16)  8.89 us
    all_gather x1, blocking collectives, gram_body(): all_energies = lax.all_gather(energies, 'samp', axis=0, tiled=True)  8.27 us
  transfers between devices with their start and end apart: 3, of which 2 were waited for; matrix products, arithmetic and copies ran while one was open for 3% of the time, Pallas kernels for 0%

commit v1 on v0

--- a/solution.py
+++ b/solution.py
@@ -30,10 +30,10 @@
     widened = slab.astype(jnp.float32)
     col_mean = jnp.sum(widened, axis=0) / total_rows
     centered = ((widened - col_mean) * (1.0 / math.sqrt(total_cols))).astype(jnp.bfloat16)
-    gram = lax.psum(
-        jnp.einsum("rc,kc->rk", centered, centered, preferred_element_type=jnp.float32),
-        ("samp", "par"),
+    partial = lax.psum(
+        jnp.einsum("rc,kc->rk", centered, centered, preferred_element_type=jnp.float32), "par"
     )
+    gram = lax.psum(partial, "samp")
     all_energies = lax.all_gather(energies, "samp", axis=0, tiled=True)
     all_picks = lax.all_gather(nys_rows, "samp", axis=0, tiled=True)
     selected = (jnp.arange(groups, dtype=jnp.int32)[:, None] * samp_rows + all_picks).reshape(-1)

time: 352 us -> 319 us (0.906)
  waiting for transfers between devices: 145 us -> 106 us
  blocking collectives: 106 us -> 116 us
  starting transfers between devices: 5.59 us -> 0.3 us
    all_to_all x0 -> x1, blocking collectives: none -> 99.2 us  [gram_body(): lax.all_to_all(log_derivs, 'samp', split_axis=1, concat_axis=0, tiled=True)]
    all_gather x1, blocking collectives: 97.4 us -> 7.85 us  [gram_body(): all_picks = lax.all_gather(nys_rows, 'samp', axis=0, tiled=True)]
    psum x1, waiting for transfers between devices: 123 us -> 34.2 us  [gram_body(): lax.psum(jnp.einsum('rc,kc->rk', centered, centered, preferred_element_ty...]
    psum x0 -> x1, waiting for transfers between devices: none -> 50 us  [gram_body(): gram = lax.psum(partial, 'samp')]
    all_to_all x1 -> x0, starting transfers between devices: 5.33 us -> none  [gram_body(): lax.all_to_all(log_derivs, 'samp', split_axis=1, concat_axis=0, tiled=True)]
  transfers between devices with their start and end apart: 3 -> 3, of which waited for: 2 -> 3; matrix products, arithmetic and copies ran while one was open for 3% -> 3% of each run, Pallas kernels for 0% -> 0%
where the time goes in v1:
time: 319 us; the launch traced here: 318 us
  blocking collectives  116 us (36%)
  waiting for transfers between devices  106 us (33%)
  other arithmetic  42.9 us (13%)
  matrix products  23.5 us (7%)
  local copies, waits for them, and re-layouts  15.1 us (5%)
  between operations  13.9 us (4%)
    all_to_all x1, blocking collectives, gram_body(): lax.all_to_all(log_derivs, 'samp', split_axis=1, concat_axis=0, tiled=True)  99.2 us
    psum x1, waiting for transfers between devices, gram_body(): gram = lax.psum(partial, 'samp')  50 us
    psum x1, waiting for transfers between devices, gram_body(): lax.psum(jnp.einsum('rc,kc->rk', centered, centered, preferred_element_ty...  34.2 us
    all_gather x1, waiting for transfers between devices, gram_body(): lax.all_gather(local_update.astype(jnp.bfloat16), 'samp', axis=0, tiled=T...  22.1 us
    dot_general x1, matrix products, gram_body(): jnp.einsum('rc,kc->rk', centered, centered, preferred_element_type=jnp.fl...  11.3 us
    another operation x8, other arithmetic, factor_solve(): lax.linalg.triangular_solve(factor, middle, left_side=True, lower=True, t...  9.37 us
    all_gather x1, blocking collectives, gram_body(): all_energies = lax.all_gather(energies, 'samp', axis=0, tiled=True)  9.06 us
    another operation x1, other arithmetic  8.89 us
  transfers between devices with their start and end apart: 3, of which 3 were waited for; matrix products, arithmetic and copies ran while one was open for 3% of the time, Pallas kernels for 0%

profile of v1, /device:TPU:0, one launch (start us, length us, event | category | flops | bytes accessed | tf_op | source)
XLA Modules:
  0.0 318.0 jit_solution(13652448125382300747)
XLA Ops:
  7.2 7.6 %copy.62 = bf16[8,8,8,8192]{3,2,0,1:T(8,128)(2,1)} copy(bf16[8,8,8,8192]{3,2,1,0:T(8,128)(2,1)} %bitcast.122) | data formatting | bytes 16777216 | tf_op jit(solution)/shard_map/all_to_all | solution.py:29
  14.8 99.2 %all_to_all.13 = bf16[64,8,8192]{2,0,1:T(8,128)(2,1)S(1)} all-to-all(bf16[64,8,8192]{2,0,1:T(8,128)(2,1)} %bitcast.121), channel_id=1, replica_groups=mesh['samp'=8,'par'=4] {'samp'}, dimensions={1} | all-to-all | bytes 16777216 | tf_op jit(solution)/shard_map/all_to_all | solution.py:29
  114.0 3.2 %copy-done = bf16[64,8,8192]{2,0,1:T(8,128)(2,1)} copy-done((bf16[64,8,8192]{2,0,1:T(8,128)(2,1)}, bf16[64,8,8192]{2,0,1:T(8,128)(2,1)S(1)}, u32[]{:S(2)}) %copy-start) | copy-done | bytes 8388632
  117.2 2.1 convert_reduce_fusion
  119.4 8.9 %multiply_convert_fusion = bf16[64,8,8192]{2,0,1:T(8,128)(2,1)} fusion(bf16[64,8,8192]{2,0,1:T(8,128)(2,1)} %copy-done, f32[8192]{0:T(1024)S(1)} %broadcast_multiply_fusion), kind=kLoop, calls=%fused_computation.5 | loop fusion | flops 16777216 | bytes 16809984 | tf_op jit(solution)/shard_map/convert.2
  128.3 11.3 %fusion.73 = f32[512,512]{1,0:T(8,128)} fusion(bf16[512,8192]{1,0:T(8,128)(2,1)} %bitcast.123), kind=kOutput, calls=%fused_computation.118 | convolution fusion | flops 4294967296 | bytes 9437184 | tf_op jit(solution)/shard_map/rc,kc->rk/dot_general | solution.py:34
  139.6 7.8 %all-gather.1 = s32[8,1,8]{2,1,0:T(1,128)S(1)} all-gather(s32[1,1,8]{2,1,0:T(1,128)S(1)} %bitcast.126), channel_id=1, replica_groups=mesh['samp'=8,'par'=4] {'samp'}, dimensions={0}, use_global_device_ids=true | all-gather | bytes 288 | tf_op jit(solution)/shard_map/all_gather | solution.py:38
  147.7 9.1 %all-gather = f32[8,64,8]{1,2,0:T(8,128)S(1)} all-gather(f32[1,64,8]{1,2,0:T(8,128)S(1)} %bitcast.125), channel_id=1, replica_groups=mesh['samp'=8,'par'=4] {'samp'}, dimensions={0}, use_global_device_ids=true | all-gather | bytes 18432 | tf_op jit(solution)/shard_map/all_gather | solution.py:37
  156.9 34.2 %all-reduce.3.cloned.1.call-done = f32[512,512]{1,0:T(8,128)} async-done(((f32[512,512]{1,0:T(8,128)}), f32[512,512]{1,0:T(8,128)}) %all-reduce.3.cloned.1.call-update) | async-done | bytes 1048592 | tf_op jit(solution)/shard_map/psum | solution.py:33
  191.3 8.9 %fusion.1 = bf16[512,8192]{1,0:T(8,128)(2,1)} fusion(bf16[64,8,8192]{2,0,1:T(8,128)(2,1)} %copy-done, f32[8192]{0:T(1024)S(1)} %broadcast_multiply_fusion), kind=kLoop, calls=%fused_computation.4 | loop fusion | flops 16777216 | bytes 16809984 | tf_op jit(solution)/shard_map/convert_element_type | solution.py:32
  200.2 50.0 %all-reduce.5.cloned.1.call-done = f32[512,512]{1,0:T(8,128)} async-done(((f32[512,512]{1,0:T(8,128)}), f32[512,512]{1,0:T(8,128)}) %all-reduce.5.cloned.1.call-update) | async-done | bytes 1048592 | tf_op jit(solution)/shard_map/psum | solution.py:36
  250.2 1.6 copy.48
  251.9 0.7 gather_fusion
  253.8 5.8 %cholesky.33 = f32[64,64]{1,0:T(8,128)S(1)} custom-call(f32[64,64]{1,0:T(8,128)S(1)} %fusion.29), custom_call_target="Cholesky" | custom-call | tf_op jit(solution)/shard_map/jit(cholesky)/cholesky | solution.py:42
  259.7 0.6 compare_reduce_fusion.3
  260.3 0.7 fusion.20
  261.0 4.9 %custom-call.24 = f32[1,64,64]{1,2,0:T(8,128)S(1)} custom-call(f32[1,64,64]{2,1,0:T(8,128)S(1)} %fusion.20), custom_call_target="InvertDiagBlocksLowerTriangular" | custom-call | tf_op jit(solution)/shard_map/triangular_solve/custom-call.3 | solution.py:13
  267.0 1.8 convolution_add_fusion.4
  269.0 0.7 cholesky.94
  269.8 0.6 compare_reduce_fusion.2
  270.4 0.6 fusion.44
  272.5 0.7 cholesky.105
  273.2 0.6 compare_reduce_fusion.1
  273.9 0.6 fusion.45
  274.5 0.6 custom-call.30
  277.5 0.7 cholesky.116
  278.3 0.6 compare_reduce_fusion
  279.0 0.6 fusion.46
  280.8 5.2 %convolution_convert_fusion = bf16[8192,8]{0,1:T(8,128)(2,1)} fusion(bf16[512,8192]{1,0:T(8,128)(2,1)} %fusion.1, f32[512,8]{0,1:T(8,128)S(1)} %convolution_add_fusion.1), kind=kOutput, calls=%fused_computation.6 | convolution fusion | flops 67178496 | bytes 8536064 | tf_op jit(solution)/shard_map/rc,rv->cv/dot_general | solution.py:66
  286.1 0.7 constant_dynamic-slice_fusion
  286.7 22.1 %all-gather.4.cloned.1.call-done = bf16[65536,8]{0,1:T(8,128)(2,1)} async-done(((bf16[8192,8]{0,1:T(8,128)(2,1)}), bf16[65536,8]{0,1:T(8,128)(2,1)}) %all-gather.4.cloned.1.call-update) | async-done | bytes 1048592 | tf_op jit(solution)/shard_map/all_gather | solution.py:69
  308.8 2.7 convert_element_type.49
  (64 shorter events, 8.4 us)
Async XLA Ops:
  7.2 183.9 %all-reduce.3.cloned.1.call-start = ((), (), s32[]{:S(2)}) async-start(), calls=%async_computation.1 | async-start | bytes 2097152 | tf_op jit(solution)/shard_map/psum | solution.py:33
  114.0 3.2 %copy-start = (bf16[64,8,8192]{2,0,1:T(8,128)(2,1)}, bf16[64,8,8192]{2,0,1:T(8,128)(2,1)S(1)}, u32[]{:S(2)}) copy-start(bf16[64,8,8192]{2,0,1:T(8,128)(2,1)S(1)} %all_to_all.13) | copy-start | bytes 25165828
  128.3 11.4 %copy-start.3 = (s32[1,8]{1,0:T(1,128)S(1)}, s32[1,8]{1,0:T(1,128)}, u32[]{:S(2)}) copy-start(s32[1,8]{1,0:T(1,128)} %param.14) | copy-start | bytes 100
  128.3 19.5 %copy-start.2 = (f32[64,8]{0,1:T(8,128)S(1)}, f32[64,8]{0,1:T(8,128)}, u32[]{:S(2)}) copy-start(f32[64,8]{0,1:T(8,128)} %param.13) | copy-start | bytes 6148
  139.6 110.6 %all-reduce.5.cloned.1.call-start = ((), (), s32[]{:S(2)}) async-start(), calls=%async_computation.2 | async-start | bytes 2097152 | tf_op jit(solution)/shard_map/psum | solution.py:36
  191.1 117.8 %all-gather.4.cloned.1.call-start = ((), (), s32[]{:S(2)}) async-start(), calls=%async_computation.3 | async-start | bytes 1179648 | tf_op jit(solution)/shard_map/all_gather | solution.py:69
  250.2 26.5 %copy-start.1 = (f32[512,512]{1,0:T(8,128)S(1)}, f32[512,512]{1,0:T(8,128)}, u32[]{:S(2)}) copy-start(f32[512,512]{1,0:T(8,128)} %all-reduce.5.cloned.1.call-done) | copy-start | bytes 3145732
Sparse Core Ops, SparseCore 0:
  139.7 51.3 all-reduce.2
  194.2 55.9 all-reduce.4
  286.2 22.6 all-gather.3
